TPU v7x, 32 devices: a whole 2x2x4 slice. The times are simulated.
32 devices in a mesh: grp: 2 (over y), seq: 16 (over z, x, core).
Axes of the slice: x: 2, y: 2, z: 4, core: 2. Of those that a mesh axis runs over, the one named last changes fastest.
Arguments:
- frames: bfloat16 [4, 10240, 1280], P('grp', 'seq'), parts along dimension 0, may hold values from -120 to 120
- dec_states: bfloat16 [2, 256, 1280], P(None, 'grp'), parts along dimension 1, may hold values from -6 to 6
- w_query: bfloat16 [1280, 1280], P(None, 'seq'), may hold values from -0.15625 to 0.15625
- w_keyval: bfloat16 [1280, 2560], replicated, may hold values from -0.15625 to 0.15625
- w_output: bfloat16 [1280, 1280], P(None, 'seq'), may hold values from -0.15625 to 0.15625
- head_slope: float32 [20], replicated, may hold values from 0.3 to 12
- lengths: int32 [4, 16], P('grp'), parts along dimension 0, may hold values from 128 to 640, as said below
- positions: int32 [2, 256], P(None, 'grp'), parts along dimension 1, may hold values from 0 to 15
Outputs:
- attended: bfloat16 [2, 256, 1280], P(None, 'grp', 'seq'), parts along dimension 1
There are 2 independent parts, one for each index of `grp`. A program takes and returns all parts, laid end to end along the dimension named above; an argument that names none is the same for every part. Nothing has to cross between parts.
Inputs may be any that keep to these rules, and one draw needn't show every extreme that they name: `lengths`: every step has one block of exactly 640 valid frames.
All inputs are finite; a program needn't handle non-finite values.
Results may differ from a plain program's by a relative error of at most 0.005.
The roundings to bfloat16 on the way count: a program that leaves them out, or rounds other values in their place, can miss the bound.
Values may be sent and summed in bfloat16 or wider, within the bound.
A program may use at most 128 MiB of HBM per device.

v0:
```python
import functools
import math

import jax
import jax.numpy as jnp
from jax import lax
from jax.sharding import PartitionSpec as P


def block_partial(
    queries,
    block_keys,
    block_values,
    length_now,
    slot_place,
    age_steps,
    row_positions,
    head_slope,
    devices,
):
    query_rows, head_count, head_size = queries.shape
    frame_count = block_keys.shape[0]
    keys_split = block_keys.reshape(frame_count, head_count, head_size)
    scores = jnp.einsum(
        "qhd,jhd->hqj", queries, keys_split, preferred_element_type=jnp.float32
    ) / math.sqrt(head_size)
    distance = (
        jnp.abs(row_positions.astype(jnp.float32) - slot_place.astype(jnp.float32)) / devices
        + age_steps
    )
    scores = scores - head_slope[:, None, None] * distance[None, :, None]
    valid = lax.broadcasted_iota(jnp.int32, (1, 1, frame_count), 2) < length_now
    scores = jnp.where(valid, scores, -jnp.inf)
    row_peak = jnp.max(scores, axis=2)
    weights = jnp.exp(scores - row_peak[:, :, None]).astype(jnp.bfloat16)
    row_total = jnp.sum(weights.astype(jnp.float32), axis=2)
    values_split = block_values.reshape(frame_count, head_count, head_size)
    row_context = jnp.einsum(
        "hqj,jhd->qhd", weights, values_split, preferred_element_type=jnp.float32
    )
    return (row_peak.T, row_total.T, row_context.reshape(query_rows, head_count * head_size))


def rescale(row_context, factors, head_count):
    query_rows = row_context.shape[0]
    spread_rows = row_context.reshape(query_rows, head_count, -1) * factors[:, :, None]
    return spread_rows.reshape(query_rows, -1)


def combine_parts(head_count, earlier, later):
    peak_one, total_one, context_one = earlier
    peak_two, total_two, context_two = later
    row_top = jnp.maximum(peak_one, peak_two)
    scale_one = jnp.exp(peak_one - row_top)
    scale_two = jnp.exp(peak_two - row_top)
    merged_total = total_one * scale_one + total_two * scale_two
    merged_context = rescale(context_one, scale_one, head_count) + rescale(
        context_two, scale_two, head_count
    )
    return (row_top, merged_total, merged_context)


def local(frames, dec_states, w_query, w_keyval, w_output, head_slope, lengths, positions):
    devices = lax.axis_size("seq")
    own_index = lax.axis_index("seq")
    step_count, frame_count, model_width = frames.shape
    query_rows = dec_states.shape[1]
    head_count = head_slope.shape[0]
    head_size = model_width // head_count
    frame_rows = frames.reshape(step_count * frame_count, model_width)
    keyval = jnp.dot(frame_rows, w_keyval, preferred_element_type=jnp.float32).astype(jnp.bfloat16)
    block_keys = keyval[:, :model_width].reshape(step_count, frame_count, model_width)
    block_values = keyval[:, model_width:].reshape(step_count, frame_count, model_width)
    dec_rows = dec_states.reshape(step_count * query_rows, model_width)
    local_query = jnp.dot(dec_rows, w_query, preferred_element_type=jnp.float32).astype(
        jnp.bfloat16
    )
    queries = lax.all_gather(local_query, "seq", axis=1, tiled=True)
    queries = queries.reshape(step_count, query_rows, head_count, head_size)
    combine = functools.partial(combine_parts, head_count)
    slot_place = (own_index + 1) % devices
    results = []
    for step_now in range(step_count):
        running = None
        for older_step in range(step_now + 1):
            partial_now = block_partial(
                queries[step_now],
                block_keys[older_step],
                block_values[older_step],
                lengths[older_step, own_index],
                slot_place,
                float(step_now - older_step),
                positions[step_now],
                head_slope,
                devices,
            )
            running = partial_now if running is None else combine(running, partial_now)
        row_peak, row_total, row_context = running
        row_top = lax.pmax(row_peak, "seq")
        factors = jnp.exp(row_peak - row_top)
        row_total, row_context = lax.psum(
            (row_total * factors, rescale(row_context, factors, head_count)), "seq"
        )
        context = row_context.reshape(query_rows, head_count, head_size) / row_total[:, :, None]
        context = context.reshape(query_rows, model_width).astype(jnp.bfloat16)
        results.append(
            jnp.dot(context, w_output, preferred_element_type=jnp.float32).astype(jnp.bfloat16)
        )
    return jnp.stack(results)


def solution(mesh):
    return jax.shard_map(
        local,
        mesh=mesh,
        in_specs=(
            P("grp", "seq", None),
            P(None, "grp", None),
            P(None, "seq"),
            P(),
            P(None, "seq"),
            P(),
            P("grp", None),
            P(None, "grp"),
        ),
        out_specs=P(None, "grp", "seq"),
        check_vma=False,
    )
```

profile of v0, /device:TPU:27, one launch (start us, length us, event | category | flops | bytes accessed | tf_op | source)
XLA Modules:
  0.0 256.1 jit_solution(2014881977530584230)
XLA Ops:
  6.5 0.8 broadcast_add_fusion
  7.4 0.8 multiply_bitcast_fusion.1
  8.2 1.4 constant_dynamic-slice_fusion.1
  9.6 0.6 iota_compare_fusion.1
  10.3 10.8 %convolution_convert_fusion = bf16[1280,2560]{1,0:T(8,128)(2,1)S(1)} fusion(bf16[1280,1280]{1,0:T(8,128)(2,1)S(1)} %bitcast.89, bf16[1280,2560]{1,0:T(8,128)(2,1)} %param.11), kind=kOutput, calls=%fused_computation | convolution fusion | flops 8391884800 | bytes 16384000 | tf_op jit(solution)/shard_map/dot_general | solution.py:71
  21.1 2.8 %fusion.18 = (bf16[640,1280]{1,0:T(8,128)(2,1)}, bf16[640,1280]{1,0:T(8,128)(2,1)}, bf16[640,1280]{1,0:T(8,128)(2,1)}, bf16[640,1280]{1,0:T(8,128)(2,1)}) fusion(bf16[1280,2560]{1,0:T(8,128)(2,1)S(1)} %convolution_convert_fusion), kind=kLoop, calls=%fused_computation.53 | loop fusion | bytes 13107200 | tf_op jit(solution)/shard_map/slice | solution.py:89
  23.9 3.5 %copy.16 = bf16[640,1280]{0,1:T(8,128)(2,1)} copy(bf16[640,1280]{1,0:T(8,128)(2,1)} %get-tuple-element.26) | data formatting | bytes 3276800 | tf_op jit(solution)/shard_map/slice | solution.py:88
  27.4 1.4 convolution_convert_fusion.1
  28.9 18.6 %all_gather.3 = bf16[256,1280]{0,1:T(8,128)(2,1)S(1)} all-gather(bf16[256,80]{0,1:T(8,128)(2,1)S(1)} %convolution_convert_fusion.1), channel_id=1, replica_groups=mesh['grp'=2,'seq'=16] {'seq'}, dimensions={1}, use_global_device_ids=true | all-gather | bytes 696320 | tf_op jit(solution)/shard_map/all_gather | solution.py:78
  47.4 0.9 fusion.19
  48.4 0.6 iota_compare_fusion
  49.0 3.5 %copy.17 = bf16[640,1280]{0,1:T(8,128)(2,1)} copy(bf16[640,1280]{1,0:T(8,128)(2,1)} %get-tuple-element.25) | data formatting | bytes 3276800 | tf_op jit(solution)/shard_map/slice | solution.py:88
  52.6 2.7 %fusion.20 = f32[20,128,640]{2,1,0:T(8,128)S(1)} fusion(bf16[128,20,64]{0,2,1:T(8,128)(2,1)} %bitcast.98, bf16[640,20,64]{0,2,1:T(8,128)(2,1)} %bitcast.92), kind=kOutput, calls=%fused_computation.55 | convolution fusion | flops 209715200 | bytes 8519680 | tf_op jit(solution)/shard_map/qhd,jhd->hqj/dot_general | solution.py:24
  55.4 1.6 fusion.2
  57.0 1.0 copy-done.3
  57.9 0.3 copy-done.9
  58.2 4.6 %fusion = (f32[20,128]{1,0:T(8,128)S(1)}, f32[20,128]{1,0:T(8,128)S(1)}, f32[20,128,640]{2,1,0:T(8,128)}) fusion(f32[20,128]{1,0:T(8,128)S(1)} %get-tuple-element.33, pred[640]{0:T(1024)(128)(4,1)S(1)} %iota_compare_fusion.1, f32[20,128]{1,0:T(8,128)S(1)} %get-tuple-element.31, f32[20,128,640]{2,1,0:T(8,128)S(1)} %fusion.20, ...), kind=kOutput, calls=%fused_computation.10 | convolution fusion | flops 222817280 | bytes 15114880 | tf_op jit(solution)/shard_map/qhd,jhd->hqj/dot_general | solution.py:24
  62.8 2.0 convert_reduce_fusion
  64.9 3.5 %copy.15 = bf16[640,1280]{0,1:T(8,128)(2,1)} copy(bf16[640,1280]{1,0:T(8,128)(2,1)} %get-tuple-element.23) | data formatting | bytes 3276800 | tf_op jit(solution)/shard_map/slice | solution.py:89
  68.4 3.5 %copy.18 = bf16[640,1280]{0,1:T(8,128)(2,1)} copy(bf16[640,1280]{1,0:T(8,128)(2,1)} %get-tuple-element.24) | data formatting | bytes 3276800 | tf_op jit(solution)/shard_map/slice | solution.py:89
  71.9 7.1 %convert_reduce_fusion.2 = (f32[20,128]{1,0:T(8,128)S(1)}, f32[20,128]{1,0:T(8,128)S(1)}) fusion(f32[20,128]{1,0:T(8,128)S(1)} %get-tuple-element.7, f32[20,128]{1,0:T(8,128)S(1)} %get-tuple-element.33, f32[20,128,640]{2,1,0:T(8,128)} %get-tuple-element.36, pred[640]{0:T(1024)(128)(4,1)S(1)} %iota_compare_fusion.1, f32[20,128]{1,0:T(8,128)S(1)} %get-tuple-element.8, ...), kind=kLoop, calls=%fused_computation.7 | loop fusion | flops 22932480 | bytes 13169280 | tf_op jit(solution)/shard_map/reduce_sum | solution.py:36
  79.0 58.4 %all-reduce.2 = (f32[128,20]{0,1:T(8,128)S(1)}, f32[128,20]{0,1:T(8,128)S(1)}) all-reduce(f32[128,20]{0,1:T(8,128)S(1)} %bitcast_maximum_fusion, f32[128,20]{0,1:T(8,128)S(1)} %bitcast.104), channel_id=1, replica_groups=mesh['grp'=2,'seq'=16] {'seq'}, use_global_device_ids=true, to_apply=%region_7.8 | all-reduce | flops 5120 | bytes 40960 | tf_op jit(solution)/shard_map/pmax | solution.py:99
  137.4 6.2 %fusion.3 = f32[128,20,64]{0,2,1:T(8,128)} fusion(bf16[640,20,64]{0,2,1:T(8,128)(2,1)} %bitcast.94, f32[128,20]{0,1:T(8,128)S(1)} %get-tuple-element.38, f32[20,128,640]{2,1,0:T(8,128)} %get-tuple-element.36, f32[20,128]{1,0:T(8,128)S(1)} %get-tuple-element.7, f32[20,128]{1,0:T(8,128)S(1)} %get-tuple-element.33, pred[640]{0:T(1024)(128)(4,1)S(1)} %iota_compare_fusion.1), kind=kOutput, calls=%fused_computation.16 | convolution fusion | flops 218071040 | bytes 8878720 | tf_op jit(solution)/shard_map/hqj,jhd->qhd/dot_general | solution.py:38
  143.6 4.3 %fusion.7 = f32[128,20,64]{0,2,1:T(8,128)S(1)} fusion(bf16[640,20,64]{0,2,1:T(8,128)(2,1)S(1)} %bitcast.96, f32[128,20]{0,1:T(8,128)S(1)} %get-tuple-element.20, f32[20,128,640]{2,1,0:T(8,128)} %copy-done.2, f32[20,128]{1,0:T(8,128)S(1)} %get-tuple-element.34, f32[20,128]{1,0:T(8,128)S(1)} %get-tuple-element.32, pred[640]{0:T(1024)(128)(4,1)S(1)} %iota_compare_fusion), kind=kOutput, calls=%fused_computation.20 | convolution fusion | flops 218071040 | bytes 8878720 | tf_op jit(solution)/shard_map/hqj,jhd->qhd/dot_general | solution.py:38
  147.9 0.3 copy-done.4
  148.2 0.7 slice-done.1
  149.0 2.9 %fusion.6 = f32[128,20,64]{0,2,1:T(8,128)} fusion(f32[128,20,64]{0,2,1:T(8,128)S(1)} %fusion.7, bf16[640,20,64]{0,2,1:T(8,128)(2,1)S(1)} %bitcast.95, f32[128,20]{0,1:T(8,128)S(1)} %get-tuple-element.19, f32[128,20]{0,1:T(8,128)S(1)} %get-tuple-element.18, f32[20,128,640]{2,1,0:T(8,128)S(1)} %bitcast.91, f32[20,128]{1,0:T(8,128)S(1)} %get-tuple-element.8, ...), kind=kOutput, calls=%fused_computation.19 | convolution fusion | flops 218398720 | bytes 9544320 | tf_op jit(solution)/shard_map/hqj,jhd->qhd/dot_general | solution.py:38
  151.9 58.0 %all-reduce = (f32[128,20]{0,1:T(8,128)S(1)}, f32[128,20]{0,1:T(8,128)S(1)}) all-reduce(f32[128,20]{0,1:T(8,128)S(1)} %get-tuple-element.17, f32[128,20]{0,1:T(8,128)S(1)} %get-tuple-element.37), channel_id=1, replica_groups=mesh['grp'=2,'seq'=16] {'seq'}, use_global_device_ids=true, to_apply=%region_11.12 | all-reduce | flops 5120 | bytes 40960 | tf_op jit(solution)/shard_map/psum | solution.py:101
  209.9 35.9 %all-reduce.5.cloned.1.call-done = (f32[128,1280]{0,1:T(8,128)}, f32[128,1280]{0,1:T(8,128)}) async-done(((f32[128,1280]{0,1:T(8,128)}, f32[128,1280]{0,1:T(8,128)}), (f32[128,1280]{0,1:T(8,128)}, f32[128,1280]{0,1:T(8,128)})) %all-reduce.5.cloned.1.call-update) | async-done | bytes 1310736 | tf_op jit(solution)/shard_map/psum | solution.py:101
  245.8 1.1 fusion.11
  247.2 1.1 fusion.10
  248.6 0.6 pad_maximum_fusion
  (32 shorter events, 0.6 us)
Async XLA Ops:
  6.5 3.7 %copy-start = (bf16[2,640,1280]{2,1,0:T(8,128)(2,1)S(1)}, bf16[2,640,1280]{2,1,0:T(8,128)(2,1)}, u32[]{:S(2)}) copy-start(bf16[2,640,1280]{2,1,0:T(8,128)(2,1)} %param.8) | copy-start | bytes 9830404
  6.5 239.3 %all-reduce.5.cloned.1.call-start = ((), (), s32[]{:S(2)}) async-start(), calls=%async_computation | async-start | bytes 2621440 | tf_op jit(solution)/shard_map/psum | solution.py:101
  21.1 6.3 %copy-start.10 = (bf16[1280,80]{0,1:T(8,128)(2,1)S(1)}, bf16[1280,80]{0,1:T(8,128)(2,1)}, u32[]{:S(2)}) copy-start(bf16[1280,80]{0,1:T(8,128)(2,1)} %param.10) | copy-start | bytes 614404
  47.4 7.9 %copy-start.11 = (f32[20]{0:T(128)S(1)}, f32[20]{0:T(128)}, u32[]{:S(2)}) copy-start(f32[20]{0:T(128)} %param.13) | copy-start | bytes 244
  52.5 2.9 %copy-start.6 = (bf16[640,1280]{0,1:T(8,128)(2,1)S(1)}, bf16[640,1280]{0,1:T(8,128)(2,1)}, u32[]{:S(2)}) copy-start(bf16[640,1280]{0,1:T(8,128)(2,1)} %copy.17) | copy-start | bytes 4915204
  52.5 2.9 %copy-start.7 = (bf16[128,1280]{0,1:T(8,128)(2,1)S(1)}, bf16[128,1280]{0,1:T(8,128)(2,1)}, u32[]{:S(2)}) copy-start(bf16[128,1280]{0,1:T(8,128)(2,1)} %get-tuple-element.28) | copy-start | bytes 983044
  55.3 7.5 %copy-start.1 = (f32[20,128,640]{2,1,0:T(8,128)}, f32[20,128,640]{2,1,0:T(8,128)S(1)}, u32[]{:S(2)}) copy-start(f32[20,128,640]{2,1,0:T(8,128)S(1)} %fusion.20) | copy-start | bytes 19660804
  55.3 2.6 %copy-start.3 = (bf16[640,1280]{0,1:T(8,128)(2,1)S(1)}, bf16[640,1280]{0,1:T(8,128)(2,1)}, u32[]{:S(2)}) copy-start(bf16[640,1280]{0,1:T(8,128)(2,1)} %copy.16) | copy-start | bytes 4915204
  55.3 2.9 %copy-start.9 = (bf16[128,1280]{0,1:T(8,128)(2,1)S(1)}, bf16[128,1280]{0,1:T(8,128)(2,1)}, u32[]{:S(2)}) copy-start(bf16[128,1280]{0,1:T(8,128)(2,1)} %get-tuple-element.27) | copy-start | bytes 983044
  57.0 5.9 %copy-start.2 = (f32[20,128,640]{2,1,0:T(8,128)}, f32[20,128,640]{2,1,0:T(8,128)S(1)}, u32[]{:S(2)}) copy-start(f32[20,128,640]{2,1,0:T(8,128)S(1)} %get-tuple-element.35) | copy-start | bytes 19660804
  137.4 6.3 %copy-start.5 = (bf16[640,1280]{0,1:T(8,128)(2,1)S(1)}, bf16[640,1280]{0,1:T(8,128)(2,1)}, u32[]{:S(2)}) copy-start(bf16[640,1280]{0,1:T(8,128)(2,1)} %copy.18) | copy-start | bytes 4915204
  143.6 4.3 %slice-start = ((s8[6553600]{0:T(1024)(128)(4,1)}), s8[4194304]{0:T(1024)(128)(4,1)S(1)}, s32[]{:S(2)}) async-start(s8[6553600]{0:T(1024)(128)(4,1)} %bitcast.90), calls=%async_computation.1 | async-start | bytes 8388608
  143.6 4.6 %copy-start.4 = (bf16[640,1280]{0,1:T(8,128)(2,1)S(1)}, bf16[640,1280]{0,1:T(8,128)(2,1)}, u32[]{:S(2)}) copy-start(bf16[640,1280]{0,1:T(8,128)(2,1)} %copy.15) | copy-start | bytes 4915204
  143.6 5.3 %slice-start.1 = ((s8[6553600]{0:T(1024)(128)(4,1)}), s8[2359296]{0:T(1024)(128)(4,1)S(1)}, s32[]{:S(2)}) async-start(s8[6553600]{0:T(1024)(128)(4,1)} %bitcast.90), calls=%async_computation.2 | async-start | bytes 4718592
  149.0 98.0 %copy-start.8 = (bf16[1280,80]{0,1:T(8,128)(2,1)S(1)}, bf16[1280,80]{0,1:T(8,128)(2,1)}, u32[]{:S(2)}) copy-start(bf16[1280,80]{0,1:T(8,128)(2,1)} %param.12) | copy-start | bytes 614404
Sparse Core Ops, SparseCore 0:
  152.1 93.7 all-reduce.4
where the time goes:
time: 260 us; the launch traced here: 256 us
  blocking collectives  135 us (52%)
  waiting for transfers between devices  35.9 us (14%)
  matrix products  35 us (13%)
  local copies, waits for them, and re-layouts  21.6 us (8%)
  other arithmetic  15.1 us (6%)
  between operations  13.6 us (5%)
    pmax x1, blocking collectives, local(): row_top = lax.pmax(row_peak, 'seq')  58.4 us
    psum x1, blocking collectives, local(): lax.psum((row_total * factors, rescale(row_context, factors, head_count))...  58 us
    psum x1, waiting for transfers between devices, local(): lax.psum((row_total * factors, rescale(row_context, factors, head_count))...  35.9 us
    all_gather x1, blocking collectives, local(): queries = lax.all_gather(local_query, 'seq', axis=1, tiled=True)  18.6 us
    dot_general x3, matrix products, block_partial(): jnp.einsum('hqj,jhd->qhd', weights, values_split, preferred_element_type=...  13.5 us
    dot_general x1, matrix products, local(): jnp.dot(frame_rows, w_keyval, preferred_element_type=jnp.float32)  10.8 us
    slice x3, local copies, waits for them, and re-layouts, local(): block_values[older_step]  9.87 us
    reduce_sum x2, other arithmetic, block_partial(): row_total = jnp.sum(weights.astype(jnp.float32), axis=2)  9.08 us
  transfers between devices with their start and end apart: 1, of which 1 were waited for; matrix products, arithmetic and copies ran while one was open for 0% of the time, Pallas kernels for 0%

commit v1 on v0

v1 whole, which is shorter than its diff:
```python
import functools
import math

import jax
import jax.numpy as jnp
from jax import lax
from jax.experimental import pallas as pl
from jax.experimental.pallas import tpu as pltpu
from jax.sharding import PartitionSpec as P

MESH = pl.DeviceIdType.MESH
EXTRA = 16
MASKED = -1e30


def rows_together(ref, first, count):
    parts = [ref[first + index].astype(jnp.float32) for index in range(count)]
    return jnp.concatenate(parts, axis=0)


def await_bytes(ref, count, sem):
    part = ref.at[pl.ds(0, count)]
    pltpu.make_async_copy(part, part, sem).wait()


def kernel(
    n,
    dec_ref,
    wq_ref,
    wout_ref,
    pos_ref,
    slope_ref,
    len_ref,
    frames_hbm,
    wkv_hbm,
    out_ref,
    frames_ref,
    wkv_ref,
    k_ref,
    vt_ref,
    q_ref,
    ctx_ref,
    stat_ref,
    got_ctx,
    got_stat,
    fin_ref,
    frame_sem,
    weight_sem,
    send_sem,
    recv_sem,
):
    me = lax.axis_index("seq")
    steps, frame_count, width = frames_hbm.shape
    tokens = dec_ref.shape[0]
    per_step = tokens // steps
    heads = k_ref.shape[0]
    size = width // heads
    rows = wq_ref.shape[1]
    groups = math.gcd(heads, n)
    group_chunks = n // groups
    group_heads = heads // groups
    tile = frames_ref.shape[1]
    half = wkv_ref.shape[2]
    tiles = frames_ref.shape[0]
    per_block = frame_count // tile
    scale = 1.0 / math.sqrt(size)

    def frame_copy(index):
        return pltpu.make_async_copy(
            frames_hbm.at[index // per_block, pl.ds((index % per_block) * tile, tile)],
            frames_ref.at[index],
            frame_sem.at[index],
        )

    def weight_copy(index):
        return pltpu.make_async_copy(
            wkv_hbm.at[:, pl.ds(index * half, half)], wkv_ref.at[index], weight_sem.at[index]
        )

    frame_copy(0).start()
    weight_copy(0).start()
    for index in range(1, tiles):
        frame_copy(index).start()
    for index in range(1, wkv_ref.shape[0]):
        weight_copy(index).start()

    barrier = pltpu.get_barrier_semaphore()

    @pl.loop(1, n)
    def _(step):
        peer = lax.rem(me + step, n)
        pl.semaphore_signal(barrier, inc=1, device_id={"seq": peer}, device_id_type=MESH)

    own_query = jnp.dot(dec_ref[...], wq_ref[...], preferred_element_type=jnp.float32)
    q_ref[me] = own_query.T.astype(jnp.bfloat16)
    pl.semaphore_wait(barrier, n - 1)

    def send(src, dst, sem, peer):
        pltpu.make_async_remote_copy(
            src_ref=src,
            dst_ref=dst,
            send_sem=send_sem.at[sem],
            recv_sem=recv_sem.at[sem],
            device_id={"seq": peer},
            device_id_type=MESH,
        ).start()

    @pl.loop(1, n)
    def _(step):
        send(q_ref.at[me], q_ref.at[me], 0, lax.rem(me + step, n))

    column = lax.broadcasted_iota(jnp.int32, (frame_count, EXTRA), 1)
    place = lax.broadcasted_iota(jnp.int32, (frame_count, EXTRA), 0)
    masks = []
    for older in range(steps):
        hidden = (place >= len_ref[older, me]) & (column == 0)
        masks.append(jnp.where(hidden, MASKED, 0.0).astype(jnp.bfloat16))
    mask = jnp.concatenate(masks, axis=0)
    ones = jnp.ones((EXTRA, steps * frame_count), jnp.bfloat16)

    @pl.loop(0, heads)
    def _(head):
        k_ref[head, :, size:] = mask
        vt_ref[head, size:, :] = ones

    halves = wkv_ref.shape[0]
    half_heads = half // size
    for part in range(halves):
        weight_copy(part).wait()

        @pl.loop(0, tiles)
        def _(index):
            if part == 0:
                frame_copy(index).wait()
            keyval = jnp.dot(
                frames_ref[index], wkv_ref[part], preferred_element_type=jnp.float32
            )
            at = pl.ds(pl.multiple_of(index * tile, tile), tile)
            if part < halves // 2:
                keyval = keyval.astype(jnp.bfloat16)
                for local_head in range(half_heads):
                    head = part * half_heads + local_head
                    k_ref[head, at, 0:size] = keyval[:, local_head * size : (local_head + 1) * size]
            else:
                turned = keyval.T.astype(jnp.bfloat16)
                for local_head in range(half_heads):
                    head = (part - halves // 2) * half_heads + local_head
                    vt_ref[head, 0:size, at] = turned[local_head * size : (local_head + 1) * size]

    await_bytes(q_ref, n - 1, send_sem.at[0])
    await_bytes(q_ref, n - 1, recv_sem.at[0])

    slot_place = lax.rem(me + 1, n).astype(jnp.float32)
    distance = jnp.abs(pos_ref[...].astype(jnp.float32) - slot_place) / n
    first_row = lax.broadcasted_iota(jnp.int32, (EXTRA, tokens), 0) == 0
    query_tail = jnp.where(first_row, 1.0, 0.0).astype(jnp.bfloat16)
    token_step = lax.broadcasted_iota(jnp.int32, (1, tokens), 1) // per_step

    @pl.loop(0, groups)
    def _(turn):
        group = lax.rem(me // group_chunks + 1 + turn, groups)
        query_rows = rows_together(q_ref, group * group_chunks, group_chunks).astype(jnp.bfloat16)
        peaks, totals, contexts = [], [], []
        for local_head in range(group_heads):
            head = group * group_heads + local_head
            query = jnp.concatenate(
                [query_rows[local_head * size : (local_head + 1) * size], query_tail], axis=0
            )
            slope = slope_ref[head]
            peak = context = None
            for older in range(steps):
                first = older * per_step
                block = pl.ds(older * frame_count, frame_count)
                raw = jnp.dot(
                    k_ref[head, block, :], query[:, first:], preferred_element_type=jnp.float32
                )
                raw_peak = jnp.max(raw, axis=0, keepdims=True)
                weights = jnp.exp2((raw - raw_peak) * (scale * math.log2(math.e)))
                part_context = jnp.dot(
                    vt_ref[head, :, block],
                    weights.astype(jnp.bfloat16),
                    preferred_element_type=jnp.float32,
                )
                age = (token_step[:, first:] - older).astype(jnp.float32)
                part_peak = raw_peak * scale - slope * (distance[:, first:] + age)
                if peak is None:
                    peak, context = part_peak, part_context
                    continue
                top = jnp.maximum(peak[:, first:], part_peak)
                old_factor = jnp.exp(peak[:, first:] - top)
                new_factor = jnp.exp(part_peak - top)
                merged = context[:, first:] * old_factor + part_context * new_factor
                peak = jnp.concatenate([peak[:, :first], top], axis=1)
                context = jnp.concatenate([context[:, :first], merged], axis=1)
            peaks.append(peak)
            totals.append(context[size : size + 1])
            contexts.append(context[:size])
        stacked = jnp.concatenate(contexts, axis=0)
        for index in range(group_chunks):
            low, high = index * rows, (index + 1) * rows
            one, two = low // size, (high - 1) // size
            chunk = group * group_chunks + index
            ctx_ref[chunk] = stacked[low:high].astype(jnp.bfloat16)
            stat_ref[chunk] = jnp.concatenate(
                [peaks[one], peaks[two], totals[one], totals[two]], axis=0
            )

        @pl.loop(0, group_chunks)
        def _(index):
            chunk = group * group_chunks + lax.rem(me + index, group_chunks)

            @pl.when(chunk != me)
            def _():
                send(stat_ref.at[chunk], got_stat.at[me], 1, chunk)
                send(ctx_ref.at[chunk], got_ctx.at[me], 2, chunk)

    got_stat[me] = stat_ref[me]
    got_ctx[me] = ctx_ref[me]
    await_bytes(got_stat, n - 1, recv_sem.at[1])
    await_bytes(got_ctx, n - 1, recv_sem.at[2])
    await_bytes(stat_ref, n - 1, send_sem.at[1])
    await_bytes(ctx_ref, n - 1, send_sem.at[2])

    top = lax.fori_loop(
        1, n, lambda at, best: jnp.maximum(best, got_stat[at][0:2]), got_stat[0][0:2]
    )
    row = lax.broadcasted_iota(jnp.int32, (rows, tokens), 0)
    is_one = row + lax.rem(me * rows, size) < size

    def add(at, state):
        total, acc = state
        stat = got_stat[at]
        factor = jnp.exp(stat[0:2] - top)
        spread = jnp.where(is_one, factor[0:1], factor[1:2])
        return total + stat[2:4] * factor, acc + got_ctx[at].astype(jnp.float32) * spread

    total, acc = lax.fori_loop(
        0,
        n,
        add,
        (jnp.zeros((2, tokens), jnp.float32), jnp.zeros((rows, tokens), jnp.float32)),
    )
    fin_ref[me] = (acc / jnp.where(is_one, total[0:1], total[1:2])).astype(jnp.bfloat16)

    @pl.loop(1, n)
    def _(step):
        send(fin_ref.at[me], fin_ref.at[me], 3, lax.rem(me + step, n))

    await_bytes(fin_ref, n - 1, recv_sem.at[3])
    await_bytes(fin_ref, n - 1, send_sem.at[3])
    turned = rows_together(fin_ref, 0, n).T.astype(jnp.bfloat16)
    attended = jnp.dot(turned, wout_ref[...], preferred_element_type=jnp.float32)
    out_ref[...] = attended.astype(jnp.bfloat16)


def local(n, frames, dec_states, w_query, w_keyval, w_output, head_slope, lengths, positions):
    steps, frame_count, width = frames.shape
    per_step = dec_states.shape[1]
    tokens = steps * per_step
    heads = head_slope.shape[0]
    size = width // heads
    rows = w_query.shape[1]
    keys = steps * frame_count
    tile = math.gcd(frame_count, 128)
    half = width // 2
    vmem = pl.BlockSpec(memory_space=pltpu.VMEM)
    smem = pl.BlockSpec(memory_space=pltpu.SMEM)
    hbm = pl.BlockSpec(memory_space=pl.ANY)
    out = pl.pallas_call(
        functools.partial(kernel, n),
        out_shape=jax.ShapeDtypeStruct((tokens, rows), jnp.bfloat16),
        in_specs=[vmem, vmem, vmem, vmem, smem, smem, hbm, hbm],
        out_specs=vmem,
        scratch_shapes=[
            pltpu.VMEM((keys // tile, tile, width), jnp.bfloat16),
            pltpu.VMEM((4, width, half), jnp.bfloat16),
            pltpu.VMEM((heads, keys, size + EXTRA), jnp.bfloat16),
            pltpu.VMEM((heads, size + EXTRA, keys), jnp.bfloat16),
            pltpu.VMEM((n, rows, tokens), jnp.bfloat16),
            pltpu.VMEM((n, rows, tokens), jnp.bfloat16),
            pltpu.VMEM((n, 4, tokens), jnp.float32),
            pltpu.VMEM((n, rows, tokens), jnp.bfloat16),
            pltpu.VMEM((n, 4, tokens), jnp.float32),
            pltpu.VMEM((n, rows, tokens), jnp.bfloat16),
            pltpu.SemaphoreType.DMA((keys // tile,)),
            pltpu.SemaphoreType.DMA((4,)),
            pltpu.SemaphoreType.DMA((4,)),
            pltpu.SemaphoreType.DMA((4,)),
        ],
        compiler_params=pltpu.CompilerParams(
            collective_id=0, has_side_effects=True, vmem_limit_bytes=60 * 1024 * 1024
        ),
    )(
        dec_states.reshape(tokens, width),
        w_query,
        w_output,
        positions.reshape(1, tokens),
        head_slope,
        lengths,
        frames,
        w_keyval,
    )
    return out.reshape(steps, per_step, rows)


def solution(mesh):
    return jax.shard_map(
        functools.partial(local, mesh.shape["seq"]),
        mesh=mesh,
        in_specs=(
            P("grp", "seq", None),
            P(None, "grp", None),
            P(None, "seq"),
            P(),
            P(None, "seq"),
            P(),
            P("grp", None),
            P(None, "grp"),
        ),
        out_specs=P(None, "grp", "seq"),
        check_vma=False,
    )
```

time: 260 us -> 73.2 us (0.28); the launches traced: 256 us -> 73 us
  blocking collectives: 135 us -> 0 us
  Pallas kernels: 0 us -> 67.8 us
  waiting for transfers between devices: 35.9 us -> 0 us
  matrix products: 35 us -> 0 us
  local copies, waits for them, and re-layouts: 21.6 us -> 5.19 us
  other arithmetic: 15.1 us -> 0 us
  between operations: 13.6 us -> 0.01 us
    pallas_call x0 -> x1, Pallas kernels: none -> 67.8 us  [local(): pl.pallas_call(functools.partial(kernel, n), out_shape=jax.ShapeDtypeStru...]
    pmax x1 -> x0, blocking collectives: 58.4 us -> none  [local(): row_top = lax.pmax(row_peak, 'seq')]
    psum x1 -> x0, blocking collectives: 58 us -> none  [local(): lax.psum((row_total * factors, rescale(row_context, factors, head_count))...]
    psum x1 -> x0, waiting for transfers between devices: 35.9 us -> none  [local(): lax.psum((row_total * factors, rescale(row_context, factors, head_count))...]
    dot_general x10 -> x0, matrix products: 35 us -> none  [the longest x3 13.5 us: block_partial(): jnp.einsum('hqj,jhd->qhd', weights, values_split, preferred_element_type=...]
    all_gather x1 -> x0, blocking collectives: 18.6 us -> none  [local(): queries = lax.all_gather(local_query, 'seq', axis=1, tiled=True)]
    slice x6 -> x0, local copies, waits for them, and re-layouts: 17.8 us -> none  [the longest x3 9.87 us: local(): block_values[older_step]]
    reduce_sum x2 -> x0, other arithmetic: 9.08 us -> none  [block_partial(): row_total = jnp.sum(weights.astype(jnp.float32), axis=2)]
  transfers between devices with their start and end apart: 1 -> 0, of which waited for: 1 -> 0; matrix products, arithmetic and copies ran while one was open for 0% -> 0% of each run, Pallas kernels for 0% -> 0%
where the time goes in v1:
time: 73.2 us; the launch traced here: 73 us
  Pallas kernels  67.8 us (93%)
  local copies, waits for them, and re-layouts  5.19 us (7%)
    pallas_call x1, Pallas kernels, local(): pl.pallas_call(functools.partial(kernel, n), out_shape=jax.ShapeDtypeStru...  67.8 us
    unnamed x2, local copies, waits for them, and re-layouts  3.64 us
    reshape x1, local copies, waits for them, and re-layouts, local(): return out.reshape(steps, per_step, rows)  1.55 us

profile of v1, /device:TPU:27, one launch (start us, length us, event | category | flops | bytes accessed | tf_op | source)
XLA Modules:
  0.0 73.0 jit_solution(364337260119168721)
XLA Ops:
  0.0 1.8 %copy.9.wq_ref = bf16[1280,80]{1,0:T(8,128)(2,1)} copy(bf16[1280,80]{0,1:T(8,128)(2,1)} %param.10) | data formatting | bytes 409600 | tf_op args[2]
  1.8 1.8 %copy.10.wout_ref = bf16[1280,80]{1,0:T(8,128)(2,1)} copy(bf16[1280,80]{0,1:T(8,128)(2,1)} %param.12) | data formatting | bytes 409600 | tf_op args[4]
  3.6 67.8 %shard_map.82 = bf16[256,80]{1,0:T(8,128)(2,1)} custom-call(bf16[256,1280]{1,0:T(8,128)(2,1)} %bitcast.3, bf16[1280,80]{1,0:T(8,128)(2,1)} %copy.9.wq_ref, bf16[1280,80]{1,0:T(8,128)(2,1)} %copy.10.wout_ref, s32[1,256]{1,0:T(1,128)} %bitcast.5, f32[20]{0:T(128)} %slope_ref.1, s32[2,16]{1,0:T(2,128)} %len_ref.1, bf16[2,640,1280]{2,1,0:T(8,128)(2,1)} %frames_hbm.1, ...), custom_call_target="tpu_custom_call" | custom-call | tf_op jit(solution)/shard_map/pallas_call | solution.py:269
  71.4 1.5 %copy.11 = bf16[2,128,80]{1,2,0:T(8,128)(2,1)} copy(bf16[2,128,80]{2,1,0:T(8,128)(2,1)} %bitcast.4) | data formatting | bytes 81920 | tf_op jit(solution)/shard_map/reshape | solution.py:303

commit v2 on v1

--- a/solution.py
+++ b/solution.py
@@ -48,6 +48,7 @@
     weight_sem,
     send_sem,
     recv_sem,
+    hop_sem,
 ):
     me = lax.axis_index("seq")
     steps, frame_count, width = frames_hbm.shape
@@ -55,7 +56,7 @@
     per_step = tokens // steps
     heads = k_ref.shape[0]
     size = width // heads
-    rows = wq_ref.shape[1]
+    rows = wq_ref.shape[0]
     groups = math.gcd(heads, n)
     group_chunks = n // groups
     group_heads = heads // groups
@@ -74,7 +75,7 @@
 
     def weight_copy(index):
         return pltpu.make_async_copy(
-            wkv_hbm.at[:, pl.ds(index * half, half)], wkv_ref.at[index], weight_sem.at[index]
+            wkv_hbm.at[:, pl.ds(pl.multiple_of(index * half, half), half)], wkv_ref.at[index], weight_sem.at[index]
         )
 
     frame_copy(0).start()
@@ -91,8 +92,10 @@
         peer = lax.rem(me + step, n)
         pl.semaphore_signal(barrier, inc=1, device_id={"seq": peer}, device_id_type=MESH)
 
-    own_query = jnp.dot(dec_ref[...], wq_ref[...], preferred_element_type=jnp.float32)
-    q_ref[me] = own_query.T.astype(jnp.bfloat16)
+    own_query = lax.dot_general(
+        wq_ref[...], dec_ref[...], (((1,), (1,)), ((), ())), preferred_element_type=jnp.float32
+    )
+    q_ref[me] = own_query.astype(jnp.bfloat16)
     pl.semaphore_wait(barrier, n - 1)
 
     def send(src, dst, sem, peer):
@@ -109,43 +112,49 @@
     def _(step):
         send(q_ref.at[me], q_ref.at[me], 0, lax.rem(me + step, n))
 
-    column = lax.broadcasted_iota(jnp.int32, (frame_count, EXTRA), 1)
-    place = lax.broadcasted_iota(jnp.int32, (frame_count, EXTRA), 0)
+    column = lax.broadcasted_iota(jnp.int32, (frame_count, size + EXTRA), 1)
+    place = lax.broadcasted_iota(jnp.int32, (frame_count, size + EXTRA), 0)
     masks = []
     for older in range(steps):
-        hidden = (place >= len_ref[older, me]) & (column == 0)
+        hidden = (place >= len_ref[older, me]) & (column == size)
         masks.append(jnp.where(hidden, MASKED, 0.0).astype(jnp.bfloat16))
     mask = jnp.concatenate(masks, axis=0)
     ones = jnp.ones((EXTRA, steps * frame_count), jnp.bfloat16)
 
     @pl.loop(0, heads)
     def _(head):
-        k_ref[head, :, size:] = mask
+        k_ref[head] = mask
         vt_ref[head, size:, :] = ones
 
-    halves = wkv_ref.shape[0]
-    half_heads = half // size
-    for part in range(halves):
+    parts = wkv_ref.shape[0] // 2
+    part_heads = half // size
+
+    def project(part, index):
+        at = pl.ds(pl.multiple_of(index * tile, tile), tile)
+        keyval = jnp.dot(frames_ref[index], wkv_ref[part], preferred_element_type=jnp.float32)
+        return at, keyval.astype(jnp.bfloat16)
+
+    for index in range(tiles):
+        frame_copy(index).wait()
+
+    @pl.loop(0, parts)
+    def _(part):
         weight_copy(part).wait()
-
-        @pl.loop(0, tiles)
-        def _(index):
-            if part == 0:
-                frame_copy(index).wait()
-            keyval = jnp.dot(
-                frames_ref[index], wkv_ref[part], preferred_element_type=jnp.float32
-            )
-            at = pl.ds(pl.multiple_of(index * tile, tile), tile)
-            if part < halves // 2:
-                keyval = keyval.astype(jnp.bfloat16)
-                for local_head in range(half_heads):
-                    head = part * half_heads + local_head
-                    k_ref[head, at, 0:size] = keyval[:, local_head * size : (local_head + 1) * size]
-            else:
-                turned = keyval.T.astype(jnp.bfloat16)
-                for local_head in range(half_heads):
-                    head = (part - halves // 2) * half_heads + local_head
-                    vt_ref[head, 0:size, at] = turned[local_head * size : (local_head + 1) * size]
+        for index in range(tiles):
+            at, keyval = project(part, index)
+            for local_head in range(part_heads):
+                lanes = slice(local_head * size, (local_head + 1) * size)
+                k_ref[part * part_heads + local_head, at, 0:size] = keyval[:, lanes]
+
+    @pl.loop(0, parts)
+    def _(part):
+        weight_copy(parts + part).wait()
+        for index in range(tiles):
+            at, keyval = project(parts + part, index)
+            turned = keyval.T
+            for local_head in range(part_heads):
+                lanes = slice(local_head * size, (local_head + 1) * size)
+                vt_ref[part * part_heads + local_head, 0:size, at] = turned[lanes]
 
     await_bytes(q_ref, n - 1, send_sem.at[0])
     await_bytes(q_ref, n - 1, recv_sem.at[0])
@@ -242,15 +251,48 @@
     )
     fin_ref[me] = (acc / jnp.where(is_one, total[0:1], total[1:2])).astype(jnp.bfloat16)
 
-    @pl.loop(1, n)
+    partner = me + 1 - 2 * lax.rem(me, 2)
+    chips = n // 2
+
+    def pass_on(chunk):
+        pltpu.make_async_remote_copy(
+            src_ref=fin_ref.at[chunk],
+            dst_ref=fin_ref.at[chunk],
+            send_sem=send_sem.at[3],
+            recv_sem=recv_sem.at[3],
+            device_id={"seq": partner},
+            device_id_type=MESH,
+        ).start()
+
+    def hop(step):
+        return pltpu.make_async_remote_copy(
+            src_ref=fin_ref.at[me],
+            dst_ref=fin_ref.at[me],
+            send_sem=send_sem.at[0],
+            recv_sem=hop_sem.at[step],
+            device_id={"seq": lax.rem(me + 2 * step, n)},
+            device_id_type=MESH,
+        )
+
+    @pl.loop(1, chips)
     def _(step):
-        send(fin_ref.at[me], fin_ref.at[me], 3, lax.rem(me + step, n))
-
-    await_bytes(fin_ref, n - 1, recv_sem.at[3])
-    await_bytes(fin_ref, n - 1, send_sem.at[3])
-    turned = rows_together(fin_ref, 0, n).T.astype(jnp.bfloat16)
-    attended = jnp.dot(turned, wout_ref[...], preferred_element_type=jnp.float32)
-    out_ref[...] = attended.astype(jnp.bfloat16)
+        hop(step).start()
+
+    pass_on(me)
+
+    @pl.loop(1, chips)
+    def _(step):
+        hop(step).wait_recv()
+        pass_on(lax.rem(me - 2 * step + n, n))
+
+    await_bytes(fin_ref, chips - 1, send_sem.at[0])
+    await_bytes(fin_ref, chips, recv_sem.at[3])
+    await_bytes(fin_ref, chips, send_sem.at[3])
+    context = rows_together(fin_ref, 0, n).astype(jnp.bfloat16)
+    attended = jnp.dot(wout_ref[...], context, preferred_element_type=jnp.float32)
+    attended = attended.astype(jnp.bfloat16)
+    for step in range(steps):
+        out_ref[step] = attended[:, step * per_step : (step + 1) * per_step]
 
 
 def local(n, frames, dec_states, w_query, w_keyval, w_output, head_slope, lengths, positions):
@@ -261,19 +303,19 @@
     size = width // heads
     rows = w_query.shape[1]
     keys = steps * frame_count
-    tile = math.gcd(frame_count, 128)
-    half = width // 2
+    tile = frame_count
+    part = math.gcd(width, 256)
     vmem = pl.BlockSpec(memory_space=pltpu.VMEM)
     smem = pl.BlockSpec(memory_space=pltpu.SMEM)
     hbm = pl.BlockSpec(memory_space=pl.ANY)
     out = pl.pallas_call(
         functools.partial(kernel, n),
-        out_shape=jax.ShapeDtypeStruct((tokens, rows), jnp.bfloat16),
+        out_shape=jax.ShapeDtypeStruct((steps, rows, per_step), jnp.bfloat16),
         in_specs=[vmem, vmem, vmem, vmem, smem, smem, hbm, hbm],
         out_specs=vmem,
         scratch_shapes=[
             pltpu.VMEM((keys // tile, tile, width), jnp.bfloat16),
-            pltpu.VMEM((4, width, half), jnp.bfloat16),
+            pltpu.VMEM((2 * width // part, width, part), jnp.bfloat16),
             pltpu.VMEM((heads, keys, size + EXTRA), jnp.bfloat16),
             pltpu.VMEM((heads, size + EXTRA, keys), jnp.bfloat16),
             pltpu.VMEM((n, rows, tokens), jnp.bfloat16),
@@ -283,24 +325,25 @@
             pltpu.VMEM((n, 4, tokens), jnp.float32),
             pltpu.VMEM((n, rows, tokens), jnp.bfloat16),
             pltpu.SemaphoreType.DMA((keys // tile,)),
+            pltpu.SemaphoreType.DMA((2 * width // part,)),
             pltpu.SemaphoreType.DMA((4,)),
             pltpu.SemaphoreType.DMA((4,)),
-            pltpu.SemaphoreType.DMA((4,)),
+            pltpu.SemaphoreType.DMA((n // 2,)),
         ],
         compiler_params=pltpu.CompilerParams(
             collective_id=0, has_side_effects=True, vmem_limit_bytes=60 * 1024 * 1024
         ),
     )(
         dec_states.reshape(tokens, width),
-        w_query,
-        w_output,
+        w_query.T,
+        w_output.T,
         positions.reshape(1, tokens),
         head_slope,
         lengths,
         frames,
         w_keyval,
     )
-    return out.reshape(steps, per_step, rows)
+    return out.transpose(0, 2, 1)
 
 
 def solution(mesh):

time: 73.2 us -> 56.2 us (0.77)
  Pallas kernels: 67.8 us -> 54.6 us
  local copies, waits for them, and re-layouts: 5.19 us -> 1.4 us
    pallas_call x1, Pallas kernels: 67.8 us -> 54.6 us  [local(): pl.pallas_call(functools.partial(kernel, n), out_shape=jax.ShapeDtypeStru...]
    unnamed x2 -> x1, local copies, waits for them, and re-layouts: 3.64 us -> 1.4 us
    reshape x1 -> x0, local copies, waits for them, and re-layouts: 1.55 us -> none  [local(): return out.reshape(steps, per_step, rows)]
where the time goes in v2:
time: 56.2 us; the launch traced here: 56 us
  Pallas kernels  54.6 us (97%)
  local copies, waits for them, and re-layouts  1.4 us (2%)
    pallas_call x1, Pallas kernels, local(): pl.pallas_call(functools.partial(kernel, n), out_shape=jax.ShapeDtypeStru...  54.6 us
    unnamed x1, local copies, waits for them, and re-layouts  1.4 us

profile of v2, /device:TPU:27, one launch (start us, length us, event | category | flops | bytes accessed | tf_op | source)
XLA Modules:
  0.0 56.0 jit_solution(7165468690330310109)
XLA Ops:
  0.0 54.6 %shard_map.82 = bf16[2,80,128]{2,1,0:T(8,128)(2,1)} custom-call(bf16[256,1280]{1,0:T(8,128)(2,1)} %bitcast.5, bf16[80,1280]{1,0:T(8,128)(2,1)} %bitcast.6, bf16[80,1280]{1,0:T(8,128)(2,1)} %bitcast.7, s32[1,256]{1,0:T(1,128)} %bitcast.9, f32[20]{0:T(128)} %slope_ref.1, s32[2,16]{1,0:T(2,128)} %len_ref.1, bf16[2,640,1280]{2,1,0:T(8,128)(2,1)} %frames_hbm.1, ...), custom_call_target="tpu_custom_call" | custom-call | tf_op jit(solution)/shard_map/pallas_call | solution.py:311
  54.6 1.4 %copy.10 = bf16[2,128,80]{1,2,0:T(8,128)(2,1)} copy(bf16[2,128,80]{1,2,0:T(8,128)(2,1)} %bitcast.8) | data formatting | bytes 81920

commit v3 on v2

--- a/solution.py
+++ b/solution.py
@@ -108,9 +108,41 @@
             device_id_type=MESH,
         ).start()
 
-    @pl.loop(1, n)
-    def _(step):
-        send(q_ref.at[me], q_ref.at[me], 0, lax.rem(me + step, n))
+    partner = me + 1 - 2 * lax.rem(me, 2)
+    chips = n // 2
+
+    def pass_on(ref, chunk, sem):
+        send(ref.at[chunk], ref.at[chunk], sem, partner)
+
+    def hop(ref, step, sem, level):
+        return pltpu.make_async_remote_copy(
+            src_ref=ref.at[me],
+            dst_ref=ref.at[me],
+            send_sem=send_sem.at[sem],
+            recv_sem=hop_sem.at[level, step],
+            device_id={"seq": lax.rem(me + 2 * step, n)},
+            device_id_type=MESH,
+        )
+
+    def spread(ref, sem, level):
+        @pl.loop(1, chips)
+        def _(step):
+            hop(ref, step, sem, level).start()
+
+        pass_on(ref, me, level)
+
+    def relay(ref, sem, level):
+        @pl.loop(1, chips)
+        def _(step):
+            hop(ref, step, sem, level).wait_recv()
+            pass_on(ref, lax.rem(me - 2 * step + n, n), level)
+
+    def settle(ref, sem, level):
+        await_bytes(ref, chips - 1, send_sem.at[sem])
+        await_bytes(ref, chips, recv_sem.at[level])
+        await_bytes(ref, chips, send_sem.at[level])
+
+    spread(q_ref, 2, 0)
 
     column = lax.broadcasted_iota(jnp.int32, (frame_count, size + EXTRA), 1)
     place = lax.broadcasted_iota(jnp.int32, (frame_count, size + EXTRA), 0)
@@ -146,8 +178,7 @@
                 lanes = slice(local_head * size, (local_head + 1) * size)
                 k_ref[part * part_heads + local_head, at, 0:size] = keyval[:, lanes]
 
-    @pl.loop(0, parts)
-    def _(part):
+    def project_values(part):
         weight_copy(parts + part).wait()
         for index in range(tiles):
             at, keyval = project(parts + part, index)
@@ -156,8 +187,10 @@
                 lanes = slice(local_head * size, (local_head + 1) * size)
                 vt_ref[part * part_heads + local_head, 0:size, at] = turned[lanes]
 
-    await_bytes(q_ref, n - 1, send_sem.at[0])
-    await_bytes(q_ref, n - 1, recv_sem.at[0])
+    pl.loop(0, parts - 2)(project_values)
+    relay(q_ref, 2, 0)
+    pl.loop(parts - 2, parts)(project_values)
+    settle(q_ref, 2, 0)
 
     slot_place = lax.rem(me + 1, n).astype(jnp.float32)
     distance = jnp.abs(pos_ref[...].astype(jnp.float32) - slot_place) / n
@@ -170,19 +203,36 @@
         group = lax.rem(me // group_chunks + 1 + turn, groups)
         query_rows = rows_together(q_ref, group * group_chunks, group_chunks).astype(jnp.bfloat16)
         peaks, totals, contexts = [], [], []
-        for local_head in range(group_heads):
-            head = group * group_heads + local_head
+
+        def scores(local_head):
             query = jnp.concatenate(
                 [query_rows[local_head * size : (local_head + 1) * size], query_tail], axis=0
             )
+            return [
+                jnp.dot(
+                    k_ref[
+                        group * group_heads + local_head,
+                        pl.ds(older * frame_count, frame_count),
+                        :,
+                    ],
+                    query[:, older * per_step :],
+                    preferred_element_type=jnp.float32,
+                )
+                for older in range(steps)
+            ]
+
+        ready = scores(0)
+        for local_head in range(group_heads):
+            head = group * group_heads + local_head
+            raws = ready
+            if local_head + 1 < group_heads:
+                ready = scores(local_head + 1)
             slope = slope_ref[head]
             peak = context = None
             for older in range(steps):
                 first = older * per_step
                 block = pl.ds(older * frame_count, frame_count)
-                raw = jnp.dot(
-                    k_ref[head, block, :], query[:, first:], preferred_element_type=jnp.float32
-                )
+                raw = raws[older]
                 raw_peak = jnp.max(raw, axis=0, keepdims=True)
                 weights = jnp.exp2((raw - raw_peak) * (scale * math.log2(math.e)))
                 part_context = jnp.dot(
@@ -220,15 +270,15 @@
 
             @pl.when(chunk != me)
             def _():
-                send(stat_ref.at[chunk], got_stat.at[me], 1, chunk)
-                send(ctx_ref.at[chunk], got_ctx.at[me], 2, chunk)
+                send(stat_ref.at[chunk], got_stat.at[me], 4, chunk)
+                send(ctx_ref.at[chunk], got_ctx.at[me], 5, chunk)
 
     got_stat[me] = stat_ref[me]
     got_ctx[me] = ctx_ref[me]
-    await_bytes(got_stat, n - 1, recv_sem.at[1])
-    await_bytes(got_ctx, n - 1, recv_sem.at[2])
-    await_bytes(stat_ref, n - 1, send_sem.at[1])
-    await_bytes(ctx_ref, n - 1, send_sem.at[2])
+    await_bytes(got_stat, n - 1, recv_sem.at[4])
+    await_bytes(got_ctx, n - 1, recv_sem.at[5])
+    await_bytes(stat_ref, n - 1, send_sem.at[4])
+    await_bytes(ctx_ref, n - 1, send_sem.at[5])
 
     top = lax.fori_loop(
         1, n, lambda at, best: jnp.maximum(best, got_stat[at][0:2]), got_stat[0][0:2]
@@ -251,43 +301,9 @@
     )
     fin_ref[me] = (acc / jnp.where(is_one, total[0:1], total[1:2])).astype(jnp.bfloat16)
 
-    partner = me + 1 - 2 * lax.rem(me, 2)
-    chips = n // 2
-
-    def pass_on(chunk):
-        pltpu.make_async_remote_copy(
-            src_ref=fin_ref.at[chunk],
-            dst_ref=fin_ref.at[chunk],
-            send_sem=send_sem.at[3],
-            recv_sem=recv_sem.at[3],
-            device_id={"seq": partner},
-            device_id_type=MESH,
-        ).start()
-
-    def hop(step):
-        return pltpu.make_async_remote_copy(
-            src_ref=fin_ref.at[me],
-            dst_ref=fin_ref.at[me],
-            send_sem=send_sem.at[0],
-            recv_sem=hop_sem.at[step],
-            device_id={"seq": lax.rem(me + 2 * step, n)},
-            device_id_type=MESH,
-        )
-
-    @pl.loop(1, chips)
-    def _(step):
-        hop(step).start()
-
-    pass_on(me)
-
-    @pl.loop(1, chips)
-    def _(step):
-        hop(step).wait_recv()
-        pass_on(lax.rem(me - 2 * step + n, n))
-
-    await_bytes(fin_ref, chips - 1, send_sem.at[0])
-    await_bytes(fin_ref, chips, recv_sem.at[3])
-    await_bytes(fin_ref, chips, send_sem.at[3])
+    spread(fin_ref, 3, 1)
+    relay(fin_ref, 3, 1)
+    settle(fin_ref, 3, 1)
     context = rows_together(fin_ref, 0, n).astype(jnp.bfloat16)
     attended = jnp.dot(wout_ref[...], context, preferred_element_type=jnp.float32)
     attended = attended.astype(jnp.bfloat16)
@@ -326,9 +342,9 @@
             pltpu.VMEM((n, rows, tokens), jnp.bfloat16),
             pltpu.SemaphoreType.DMA((keys // tile,)),
             pltpu.SemaphoreType.DMA((2 * width // part,)),
-            pltpu.SemaphoreType.DMA((4,)),
-            pltpu.SemaphoreType.DMA((4,)),
-            pltpu.SemaphoreType.DMA((n // 2,)),
+            pltpu.SemaphoreType.DMA((6,)),
+            pltpu.SemaphoreType.DMA((6,)),
+            pltpu.SemaphoreType.DMA((2, n // 2)),
         ],
         compiler_params=pltpu.CompilerParams(
             collective_id=0, has_side_effects=True, vmem_limit_bytes=60 * 1024 * 1024

time: 56.2 us -> 50.1 us (0.89)
  Pallas kernels: 54.6 us -> 48.2 us
    pallas_call x1, Pallas kernels: 54.6 us -> 48.2 us  [local(): pl.pallas_call(functools.partial(kernel, n), out_shape=jax.ShapeDtypeStru...]
where the time goes in v3:
time: 50.1 us; the launch traced here: 49.6 us
  Pallas kernels  48.2 us (96%)
  local copies, waits for them, and re-layouts  1.4 us (3%)
    pallas_call x1, Pallas kernels, local(): pl.pallas_call(functools.partial(kernel, n), out_shape=jax.ShapeDtypeStru...  48.2 us
    unnamed x1, local copies, waits for them, and re-layouts  1.4 us

profile of v3, /device:TPU:27, one launch (start us, length us, event | category | flops | bytes accessed | tf_op | source)
XLA Modules:
  0.0 49.6 jit_solution(5208026440699717579)
XLA Ops:
  0.0 48.2 %shard_map.82 = bf16[2,80,128]{2,1,0:T(8,128)(2,1)} custom-call(bf16[256,1280]{1,0:T(8,128)(2,1)} %bitcast.5, bf16[80,1280]{1,0:T(8,128)(2,1)} %bitcast.6, bf16[80,1280]{1,0:T(8,128)(2,1)} %bitcast.7, s32[1,256]{1,0:T(1,128)} %bitcast.9, f32[20]{0:T(128)} %slope_ref.1, s32[2,16]{1,0:T(2,128)} %len_ref.1, bf16[2,640,1280]{2,1,0:T(8,128)(2,1)} %frames_hbm.1, ...), custom_call_target="tpu_custom_call" | custom-call | tf_op jit(solution)/shard_map/pallas_call | solution.py:327
  48.3 1.4 %copy.10 = bf16[2,128,80]{1,2,0:T(8,128)(2,1)} copy(bf16[2,128,80]{1,2,0:T(8,128)(2,1)} %bitcast.8) | data formatting | bytes 81920

commit v4 on v3

--- a/solution.py
+++ b/solution.py
@@ -43,12 +43,17 @@
     stat_ref,
     got_ctx,
     got_stat,
+    pair_ctx,
+    pair_stat,
+    sum_ctx,
+    sum_stat,
     fin_ref,
     frame_sem,
     weight_sem,
     send_sem,
     recv_sem,
     hop_sem,
+    pair_sem,
 ):
     me = lax.axis_index("seq")
     steps, frame_count, width = frames_hbm.shape
@@ -197,6 +202,42 @@
     first_row = lax.broadcasted_iota(jnp.int32, (EXTRA, tokens), 0) == 0
     query_tail = jnp.where(first_row, 1.0, 0.0).astype(jnp.bfloat16)
     token_step = lax.broadcasted_iota(jnp.int32, (1, tokens), 1) // per_step
+
+    row = lax.broadcasted_iota(jnp.int32, (rows, tokens), 0)
+
+    def pass_sums(turn):
+        group = lax.rem(me // group_chunks + 1 + turn, groups)
+        await_bytes(pair_stat, group_chunks // 2, pair_sem.at[0, turn])
+        await_bytes(pair_ctx, group_chunks // 2, pair_sem.at[1, turn])
+
+        @pl.loop(0, group_chunks // 2)
+        def _(index):
+            chunk = group * group_chunks + 2 * index + lax.rem(me, 2)
+            slot = chunk // 2
+            one, two = stat_ref[chunk], pair_stat[slot]
+            top = jnp.maximum(one[0:2], two[0:2])
+            one_factor = jnp.exp(one[0:2] - top)
+            two_factor = jnp.exp(two[0:2] - top)
+            stat = jnp.concatenate([top, one[2:4] * one_factor + two[2:4] * two_factor], axis=0)
+            is_one = row + lax.rem(chunk * rows, size) < size
+            context = ctx_ref[chunk].astype(jnp.float32) * jnp.where(
+                is_one, one_factor[0:1], one_factor[1:2]
+            ) + pair_ctx[slot].astype(jnp.float32) * jnp.where(
+                is_one, two_factor[0:1], two_factor[1:2]
+            )
+            context = context.astype(jnp.bfloat16)
+
+            @pl.when(chunk != me)
+            def _():
+                sum_stat[slot] = stat
+                sum_ctx[slot] = context
+                send(sum_stat.at[slot], got_stat.at[me // 2], 4, chunk)
+                send(sum_ctx.at[slot], got_ctx.at[me // 2], 5, chunk)
+
+            @pl.when(chunk == me)
+            def _():
+                got_stat[slot] = stat
+                got_ctx[slot] = context
 
     @pl.loop(0, groups)
     def _(turn):
@@ -264,26 +305,34 @@
                 [peaks[one], peaks[two], totals[one], totals[two]], axis=0
             )
 
-        @pl.loop(0, group_chunks)
+        @pl.loop(0, group_chunks // 2)
         def _(index):
-            chunk = group * group_chunks + lax.rem(me + index, group_chunks)
-
-            @pl.when(chunk != me)
-            def _():
-                send(stat_ref.at[chunk], got_stat.at[me], 4, chunk)
-                send(ctx_ref.at[chunk], got_ctx.at[me], 5, chunk)
-
-    got_stat[me] = stat_ref[me]
-    got_ctx[me] = ctx_ref[me]
-    await_bytes(got_stat, n - 1, recv_sem.at[4])
-    await_bytes(got_ctx, n - 1, recv_sem.at[5])
-    await_bytes(stat_ref, n - 1, send_sem.at[4])
-    await_bytes(ctx_ref, n - 1, send_sem.at[5])
+            chunk = group * group_chunks + 2 * index + 1 - lax.rem(me, 2)
+            for kind, (src, dst) in enumerate(((stat_ref, pair_stat), (ctx_ref, pair_ctx))):
+                pltpu.make_async_remote_copy(
+                    src_ref=src.at[chunk],
+                    dst_ref=dst.at[chunk // 2],
+                    send_sem=send_sem.at[kind],
+                    recv_sem=pair_sem.at[kind, turn],
+                    device_id={"seq": partner},
+                    device_id_type=MESH,
+                ).start()
+
+        @pl.when(turn > 0)
+        def _():
+            pass_sums(turn - 1)
+
+    pass_sums(groups - 1)
+    await_bytes(got_stat, chips - 1, recv_sem.at[4])
+    await_bytes(got_ctx, chips - 1, recv_sem.at[5])
+    await_bytes(sum_stat, chips - 1, send_sem.at[4])
+    await_bytes(sum_ctx, chips - 1, send_sem.at[5])
+    await_bytes(stat_ref, chips, send_sem.at[0])
+    await_bytes(ctx_ref, chips, send_sem.at[1])
 
     top = lax.fori_loop(
-        1, n, lambda at, best: jnp.maximum(best, got_stat[at][0:2]), got_stat[0][0:2]
+        1, chips, lambda at, best: jnp.maximum(best, got_stat[at][0:2]), got_stat[0][0:2]
     )
-    row = lax.broadcasted_iota(jnp.int32, (rows, tokens), 0)
     is_one = row + lax.rem(me * rows, size) < size
 
     def add(at, state):
@@ -295,7 +344,7 @@
 
     total, acc = lax.fori_loop(
         0,
-        n,
+        chips,
         add,
         (jnp.zeros((2, tokens), jnp.float32), jnp.zeros((rows, tokens), jnp.float32)),
     )
@@ -337,14 +386,19 @@
             pltpu.VMEM((n, rows, tokens), jnp.bfloat16),
             pltpu.VMEM((n, rows, tokens), jnp.bfloat16),
             pltpu.VMEM((n, 4, tokens), jnp.float32),
-            pltpu.VMEM((n, rows, tokens), jnp.bfloat16),
-            pltpu.VMEM((n, 4, tokens), jnp.float32),
+            pltpu.VMEM((n // 2, rows, tokens), jnp.bfloat16),
+            pltpu.VMEM((n // 2, 4, tokens), jnp.float32),
+            pltpu.VMEM((n // 2, rows, tokens), jnp.bfloat16),
+            pltpu.VMEM((n // 2, 4, tokens), jnp.float32),
+            pltpu.VMEM((n // 2, rows, tokens), jnp.bfloat16),
+            pltpu.VMEM((n // 2, 4, tokens), jnp.float32),
             pltpu.VMEM((n, rows, tokens), jnp.bfloat16),
             pltpu.SemaphoreType.DMA((keys // tile,)),
             pltpu.SemaphoreType.DMA((2 * width // part,)),
             pltpu.SemaphoreType.DMA((6,)),
             pltpu.SemaphoreType.DMA((6,)),
             pltpu.SemaphoreType.DMA((2, n // 2)),
+            pltpu.SemaphoreType.DMA((2, math.gcd(heads, n))),
         ],
         compiler_params=pltpu.CompilerParams(
             collective_id=0, has_side_effects=True, vmem_limit_bytes=60 * 1024 * 1024

time: 50.1 us -> 44.9 us (0.90)
  Pallas kernels: 48.2 us -> 43 us
    pallas_call x1, Pallas kernels: 48.2 us -> 43 us  [local(): pl.pallas_call(functools.partial(kernel, n), out_shape=jax.ShapeDtypeStru...]
where the time goes in v4:
time: 44.9 us; the launch traced here: 44.4 us
  Pallas kernels  43 us (96%)
  local copies, waits for them, and re-layouts  1.4 us (3%)
    pallas_call x1, Pallas kernels, local(): pl.pallas_call(functools.partial(kernel, n), out_shape=jax.ShapeDtypeStru...  43 us
    unnamed x1, local copies, waits for them, and re-layouts  1.4 us

profile of v4, /device:TPU:27, one launch (start us, length us, event | category | flops | bytes accessed | tf_op | source)
XLA Modules:
  0.0 44.4 jit_solution(7980422389815314441)
XLA Ops:
  0.0 43.0 %shard_map.82 = bf16[2,80,128]{2,1,0:T(8,128)(2,1)} custom-call(bf16[256,1280]{1,0:T(8,128)(2,1)} %bitcast.5, bf16[80,1280]{1,0:T(8,128)(2,1)} %bitcast.6, bf16[80,1280]{1,0:T(8,128)(2,1)} %bitcast.7, s32[1,256]{1,0:T(1,128)} %bitcast.9, f32[20]{0:T(128)} %slope_ref.1, s32[2,16]{1,0:T(2,128)} %len_ref.1, bf16[2,640,1280]{2,1,0:T(8,128)(2,1)} %frames_hbm.1, ...), custom_call_target="tpu_custom_call" | custom-call | tf_op jit(solution)/shard_map/pallas_call | solution.py:376
  43.0 1.4 %copy.10 = bf16[2,128,80]{1,2,0:T(8,128)(2,1)} copy(bf16[2,128,80]{1,2,0:T(8,128)(2,1)} %bitcast.8) | data formatting | bytes 81920

commit v5 on v4

--- a/solution.py
+++ b/solution.py
@@ -83,19 +83,19 @@
             wkv_hbm.at[:, pl.ds(pl.multiple_of(index * half, half), half)], wkv_ref.at[index], weight_sem.at[index]
         )
 
+    barrier = pltpu.get_barrier_semaphore()
+
+    @pl.loop(1, n)
+    def _(step):
+        peer = lax.rem(me + step, n)
+        pl.semaphore_signal(barrier, inc=1, device_id={"seq": peer}, device_id_type=MESH)
+
     frame_copy(0).start()
     weight_copy(0).start()
     for index in range(1, tiles):
         frame_copy(index).start()
     for index in range(1, wkv_ref.shape[0]):
         weight_copy(index).start()
-
-    barrier = pltpu.get_barrier_semaphore()
-
-    @pl.loop(1, n)
-    def _(step):
-        peer = lax.rem(me + step, n)
-        pl.semaphore_signal(barrier, inc=1, device_id={"seq": peer}, device_id_type=MESH)
 
     own_query = lax.dot_general(
         wq_ref[...], dec_ref[...], (((1,), (1,)), ((), ())), preferred_element_type=jnp.float32
@@ -119,28 +119,49 @@
     def pass_on(ref, chunk, sem):
         send(ref.at[chunk], ref.at[chunk], sem, partner)
 
+    columns = n // 4
+    beside = me + 2 - 4 * lax.rem(me // 2, 2)
+
     def hop(ref, step, sem, level):
         return pltpu.make_async_remote_copy(
             src_ref=ref.at[me],
             dst_ref=ref.at[me],
             send_sem=send_sem.at[sem],
             recv_sem=hop_sem.at[level, step],
-            device_id={"seq": lax.rem(me + 2 * step, n)},
+            device_id={"seq": lax.rem(me + 4 * step, n)},
             device_id_type=MESH,
         )
 
+    def cross(ref, step, sem, level):
+        chunk = lax.rem(me - 4 * step + n, n)
+        return pltpu.make_async_remote_copy(
+            src_ref=ref.at[chunk],
+            dst_ref=ref.at[chunk],
+            send_sem=send_sem.at[sem],
+            recv_sem=hop_sem.at[level, columns + step],
+            device_id={"seq": beside},
+            device_id_type=MESH,
+        )
+
     def spread(ref, sem, level):
-        @pl.loop(1, chips)
+        @pl.loop(1, columns)
         def _(step):
             hop(ref, step, sem, level).start()
 
+        cross(ref, 0, sem, level).start()
         pass_on(ref, me, level)
 
     def relay(ref, sem, level):
-        @pl.loop(1, chips)
+        @pl.loop(1, columns)
         def _(step):
             hop(ref, step, sem, level).wait_recv()
-            pass_on(ref, lax.rem(me - 2 * step + n, n), level)
+            cross(ref, step, sem, level).start()
+            pass_on(ref, lax.rem(me - 4 * step + n, n), level)
+
+        @pl.loop(0, columns)
+        def _(step):
+            cross(ref, step, sem, level).wait_recv()
+            pass_on(ref, lax.rem(beside - 4 * step + n, n), level)
 
     def settle(ref, sem, level):
         await_bytes(ref, chips - 1, send_sem.at[sem])

time: 44.9 us -> 50.1 us (1.12)
  the two profiles are of different devices: /device:TPU:27 before, /device:TPU:0 now
where the time goes in v5:
time: 50.1 us; the launch traced here: 49.9 us
  Pallas kernels  48.5 us (97%)
  local copies, waits for them, and re-layouts  1.4 us (3%)
    pallas_call x1, Pallas kernels, local(): pl.pallas_call(functools.partial(kernel, n), out_shape=jax.ShapeDtypeStru...  48.5 us
    unnamed x1, local copies, waits for them, and re-layouts  1.4 us

profile of v5, /device:TPU:0, one launch (start us, length us, event | category | flops | bytes accessed | tf_op | source)
XLA Modules:
  0.0 49.9 jit_solution(13905372235436127527)
XLA Ops:
  0.0 48.5 %shard_map.82 = bf16[2,80,128]{2,1,0:T(8,128)(2,1)} custom-call(bf16[256,1280]{1,0:T(8,128)(2,1)} %bitcast.5, bf16[80,1280]{1,0:T(8,128)(2,1)} %bitcast.6, bf16[80,1280]{1,0:T(8,128)(2,1)} %bitcast.7, s32[1,256]{1,0:T(1,128)} %bitcast.9, f32[20]{0:T(128)} %slope_ref.1, s32[2,16]{1,0:T(2,128)} %len_ref.1, bf16[2,640,1280]{2,1,0:T(8,128)(2,1)} %frames_hbm.1, ...), custom_call_target="tpu_custom_call" | custom-call | tf_op jit(solution)/shard_map/pallas_call | solution.py:397
  48.5 1.4 %copy.10 = bf16[2,128,80]{1,2,0:T(8,128)(2,1)} copy(bf16[2,128,80]{1,2,0:T(8,128)(2,1)} %bitcast.8) | data formatting | bytes 81920

commit v6 on v4

--- a/solution.py
+++ b/solution.py
@@ -171,17 +171,18 @@
         keyval = jnp.dot(frames_ref[index], wkv_ref[part], preferred_element_type=jnp.float32)
         return at, keyval.astype(jnp.bfloat16)
 
-    for index in range(tiles):
-        frame_copy(index).wait()
-
-    @pl.loop(0, parts)
-    def _(part):
+    def project_keys(part, fresh=False):
         weight_copy(part).wait()
         for index in range(tiles):
+            if fresh:
+                frame_copy(index).wait()
             at, keyval = project(part, index)
             for local_head in range(part_heads):
                 lanes = slice(local_head * size, (local_head + 1) * size)
                 k_ref[part * part_heads + local_head, at, 0:size] = keyval[:, lanes]
+
+    project_keys(0, True)
+    pl.loop(1, parts)(project_keys)
 
     def project_values(part):
         weight_copy(parts + part).wait()

time: 44.9 us -> 45.1 us (level)
  no operation moved by 1% of the time
where the time goes in v6:
time: 45.1 us; the launch traced here: 44.4 us
  Pallas kernels  43 us (95%)
  local copies, waits for them, and re-layouts  1.4 us (3%)
    pallas_call x1, Pallas kernels, local(): pl.pallas_call(functools.partial(kernel, n), out_shape=jax.ShapeDtypeStru...  43 us
    unnamed x1, local copies, waits for them, and re-layouts  1.4 us

profile of v6, /device:TPU:27, one launch (start us, length us, event | category | flops | bytes accessed | tf_op | source)
XLA Modules:
  0.0 44.4 jit_solution(6844925121533986852)
XLA Ops:
  0.0 43.0 %shard_map.82 = bf16[2,80,128]{2,1,0:T(8,128)(2,1)} custom-call(bf16[256,1280]{1,0:T(8,128)(2,1)} %bitcast.5, bf16[80,1280]{1,0:T(8,128)(2,1)} %bitcast.6, bf16[80,1280]{1,0:T(8,128)(2,1)} %bitcast.7, s32[1,256]{1,0:T(1,128)} %bitcast.9, f32[20]{0:T(128)} %slope_ref.1, s32[2,16]{1,0:T(2,128)} %len_ref.1, bf16[2,640,1280]{2,1,0:T(8,128)(2,1)} %frames_hbm.1, ...), custom_call_target="tpu_custom_call" | custom-call | tf_op jit(solution)/shard_map/pallas_call | solution.py:377
  43.0 1.4 %copy.10 = bf16[2,128,80]{1,2,0:T(8,128)(2,1)} copy(bf16[2,128,80]{1,2,0:T(8,128)(2,1)} %bitcast.8) | data formatting | bytes 81920
